TPU v7x, 32 devices: a whole 2x2x4 slice. The times are simulated.
32 devices in a mesh: tm: 2 (over y), row: 4 (over z), col: 4 (over x, core).
Axes of the slice: x: 2, y: 2, z: 4, core: 2. Of those that a mesh axis runs over, the one named last changes fastest.
Arguments:
- returns: bfloat16 [272, 16384], P('tm', ('row', 'col')), may hold values from -60 to 60
- window: int32 [1], replicated, may hold values from 200 to 256
- out_days: int32 [4], replicated, may hold values from 255 to 271
Outputs:
- correlation: bfloat16 [4, 16384, 16384], P(None, 'row', ('col', 'tm'))
Inputs may be any that keep to these rules, and one draw needn't show every extreme that they name: One window length for all days. `out_days`: days may repeat.
All inputs are finite; a program needn't handle non-finite values.
Results may differ from a plain program's by a relative error of at most 0.001.
Values may be sent and summed in bfloat16 or wider, within the bound.
A program may use at most 128 MiB of HBM per device.

v0:
```python
import jax
import jax.numpy as jnp
from jax import lax
from jax.sharding import PartitionSpec as P


def moments(mask, block):
    series = block.astype(jnp.float32)
    first = jnp.dot(mask, series, precision=lax.Precision.HIGHEST)
    second = jnp.dot(mask, series * series, precision=lax.Precision.HIGHEST)
    return (first, second)


def on_device(returns, window, out_days):
    width = window[0]
    wide = width.astype(jnp.float32)
    tm_count = lax.axis_size("tm")
    tm_index = lax.axis_index("tm")
    share = lax.axis_size("row") // lax.axis_size("col")
    local = lax.all_gather(returns, "tm", axis=0, tiled=True)
    row_series = lax.all_gather(local, "col", axis=1, tiled=True)
    block_width = row_series.shape[1]
    col_index = lax.axis_index("col")
    range_width = share * block_width
    half = range_width // tm_count
    half_start = tm_index * half
    range_start = col_index * range_width
    wanted_start = range_start + half_start
    everything = lax.all_gather(row_series, "row", axis=1, tiled=True)
    col_series = lax.dynamic_slice_in_dim(everything, wanted_start, half, 1)
    day_count = local.shape[0]
    day_ids = jnp.arange(day_count, dtype=jnp.int32)
    inside = (day_ids[None, :] <= out_days[:, None]) & (
        day_ids[None, :] > out_days[:, None] - width
    )
    mask = jnp.where(inside, 1.0, 0.0).astype(jnp.float32)
    weighted = mask.astype(jnp.bfloat16)[:, :, None] * row_series[None, :, :]
    gram = jnp.einsum("kda,db->kab", weighted, col_series, preferred_element_type=jnp.float32)
    first_rows, second_rows = moments(mask, row_series)
    first_cols, second_cols = moments(mask, col_series)
    scale_rows = lax.rsqrt((second_rows - first_rows * first_rows / wide) / wide + 1e-06)
    scale_cols = lax.rsqrt((second_cols - first_cols * first_cols / wide) / wide + 1e-06)
    cov = gram - first_rows[:, :, None] * first_cols[:, None, :] / wide
    return (cov * scale_rows[:, :, None] * scale_cols[:, None, :] / wide).astype(jnp.bfloat16)


def solution(mesh):
    return jax.shard_map(
        on_device,
        mesh=mesh,
        in_specs=(P("tm", ("row", "col")), P(), P()),
        out_specs=P(None, "row", ("col", "tm")),
        check_vma=False,
    )
```

profile of v0, /device:TPU:0, one launch (start us, length us, event | category | flops | bytes accessed | tf_op | source)
XLA Modules:
  0.0 272.3 jit_solution(1794039816676634413)
XLA Ops:
  6.5 0.0 copy-start.1
  6.5 0.0 all-gather.3.cloned.1.call-start
  6.5 12.4 %all_gather.9 = bf16[272,1024]{1,0:T(8,128)(2,1)} all-gather(bf16[136,1024]{1,0:T(8,128)(2,1)} %param.3), channel_id=1, replica_groups=mesh['tm'=2,'row'=4,'col'=4] {'tm'}, dimensions={0}, use_global_device_ids=true | all-gather | bytes 835584 | tf_op jit(solution)/shard_map/all_gather | solution.py:20
  18.9 0.0 all-gather.3.cloned.1.call-update
  18.9 0.0 all-gather.5.cloned.1.call-start
  19.0 23.7 %all-gather.3.cloned.1.call-done = bf16[272,4096]{1,0:T(8,128)(2,1)} async-done(((bf16[272,1024]{1,0:T(8,128)(2,1)}), bf16[272,4096]{1,0:T(8,128)(2,1)}) %all-gather.3.cloned.1.call-update) | async-done | bytes 2228240 | tf_op jit(solution)/shard_map/all_gather | solution.py:21
  42.7 0.0 copy-start
  42.7 0.0 all-gather.5.cloned.1.call-update
  43.5 0.7 broadcast_subtract_fusion
  44.2 0.7 select_convert_fusion
  44.9 2.7 %fusion.41 = f32[4,4096]{1,0:T(4,128)S(1)} fusion(bf16[272,4096]{1,0:T(8,128)(2,1)} %all-gather.3.cloned.1.call-done, s32[4]{0:T(128)S(1)} %broadcast_subtract_fusion, s32[4]{0:T(128)} %param.5), kind=kOutput, calls=%fused_computation.26 | convolution fusion | flops 53481728 | bytes 2293792 | tf_op jit(solution)/shard_map/dot_general | solution.py:9
  47.6 4.3 %fusion.15 = f32[4,4096]{1,0:T(4,128)S(1)} fusion(bf16[272,4096]{1,0:T(8,128)(2,1)} %all-gather.3.cloned.1.call-done, f32[4,4096]{1,0:T(4,128)S(1)} %fusion.41, f32[]{:T(128)S(6)} %convert_element_type.20, s32[4]{0:T(128)S(1)} %broadcast_subtract_fusion, s32[4]{0:T(128)} %param.5), kind=kOutput, calls=%fused_computation.10 | convolution fusion | flops 55791872 | bytes 2359332 | tf_op jit(solution)/shard_map/dot_general | solution.py:10
  51.9 150.6 %all-gather.5.cloned.1.call-done = bf16[272,16384]{1,0:T(8,128)(2,1)} async-done(((bf16[272,4096]{1,0:T(8,128)(2,1)}), bf16[272,16384]{1,0:T(8,128)(2,1)}) %all-gather.5.cloned.1.call-update) | async-done | bytes 8912912 | tf_op jit(solution)/shard_map/all_gather | solution.py:29
  202.5 0.0 copy-done.1
  202.5 1.9 fusion.35
  204.3 1.4 fusion.74
  205.7 2.6 fusion.30
  208.3 0.0 copy-done
  208.4 57.1 %divide_convert_fusion = bf16[4,4096,2048]{2,1,0:T(8,128)(2,1)} fusion(f32[4,2048]{1,0:T(4,128)S(1)} %fusion.30, f32[4,4096]{1,0:T(4,128)S(1)} %fusion.15, f32[]{:T(128)S(6)} %convert_element_type.20, f32[4,2048]{1,0:T(4,128)S(1)} %fusion.35, f32[4,4096]{1,0:T(4,128)S(1)} %fusion.41, bf16[272,4096]{1,0:T(8,128)(2,1)S(1)} %copy-done, ...), kind=kOutput, calls=%fused_computation | convolution fusion | flops 18492948480 | bytes 70649984 | tf_op jit(solution)/shard_map/kda,db->kab/dot_general | solution.py:38
Async XLA Ops:
  6.5 195.9 %copy-start.1 = (s32[4]{0:T(128)S(1)}, s32[4]{0:T(128)}, u32[]{:S(2)}) copy-start(s32[4]{0:T(128)} %param.5) | copy-start | bytes 52
  6.5 36.2 %all-gather.3.cloned.1.call-start = ((), (), s32[]{:S(2)}) async-start(), calls=%async_computation | async-start | bytes 2785280 | tf_op jit(solution)/shard_map/all_gather | solution.py:21
  18.9 183.5 %all-gather.5.cloned.1.call-start = ((), (), s32[]{:S(2)}) async-start(), calls=%async_computation.1 | async-start | bytes 11141120 | tf_op jit(solution)/shard_map/all_gather | solution.py:29
  42.7 165.7 %copy-start = (bf16[272,4096]{1,0:T(8,128)(2,1)S(1)}, bf16[272,4096]{1,0:T(8,128)(2,1)}, u32[]{:S(2)}) copy-start(bf16[272,4096]{1,0:T(8,128)(2,1)} %all-gather.3.cloned.1.call-done) | copy-start | bytes 6684676
Sparse Core Ops, SparseCore 0:
  19.1 23.5 all-gather.2
  44.3 158.1 all-gather.4
where the time goes:
time: 273 us; the launch traced here: 272 us
  waiting for transfers between devices  174 us (64%)
  matrix products  68.6 us (25%)
  between operations  14.2 us (5%)
  blocking collectives  12.4 us (5%)
    all_gather x1, waiting for transfers between devices, on_device(): everything = lax.all_gather(row_series, 'row', axis=1, tiled=True)  151 us
    dot_general x1, matrix products, on_device(): jnp.einsum('kda,db->kab', weighted, col_series, preferred_element_type=jn...  57.1 us
    all_gather x1, waiting for transfers between devices, on_device(): row_series = lax.all_gather(local, 'col', axis=1, tiled=True)  23.7 us
    all_gather x1, blocking collectives, on_device(): local = lax.all_gather(returns, 'tm', axis=0, tiled=True)  12.4 us
    dot_general x2, matrix products, moments(): second = jnp.dot(mask, series * series, precision=lax.Precision.HIGHEST)  6.9 us
  transfers between devices with their start and end apart: 2, of which 2 were waited for; matrix products, arithmetic and copies ran while one was open for 3% of the time, Pallas kernels for 0%

commit v1 on v0

v1 whole, which is shorter than its diff:
```python
import functools

import jax
import jax.numpy as jnp
from jax import lax
from jax.experimental import pallas as pl
from jax.experimental.pallas import tpu as pltpu
from jax.sharding import PartitionSpec as P

MESH = pl.DeviceIdType.MESH


def gather_kernel(T, R, C, x_ref, row_ref, col_ref, line, line_send, line_recv,
                  row_send, row_recv, twin_send, twin_recv, col_send, col_recv, local_sem):
    t, r, c = lax.axis_index("tm"), lax.axis_index("row"), lax.axis_index("col")
    n = R // T
    core = lax.rem(c, 2)
    twin = c + 1 - 2 * core
    chips = C // 2

    def to(tt, rr, cc):
        return {"tm": tt, "row": rr, "col": cc}

    barrier = pltpu.get_barrier_semaphore()
    for d in range(1, T * C):
        flat = lax.rem(t * C + c + d, T * C)
        pl.semaphore_signal(barrier, inc=1, device_id=to(flat // C, r, lax.rem(flat, C)), device_id_type=MESH)

    @pl.when(r > 0)
    def _():
        pl.semaphore_signal(barrier, inc=1, device_id=to(t, r - 1, c), device_id_type=MESH)

    @pl.when(r < R - 1)
    def _():
        pl.semaphore_signal(barrier, inc=1, device_id=to(t, r + 1, c), device_id_type=MESH)

    inner = jnp.logical_and(r > 0, r < R - 1)
    pl.semaphore_wait(barrier, T * C + inner.astype(jnp.int32) if R > 1 else T * C - 1)

    def rdma(src, dst, send, recv, device):
        return pltpu.make_async_remote_copy(src_ref=src, dst_ref=dst, send_sem=send, recv_sem=recv,
                                            device_id=device, device_id_type=MESH)

    def line_copy(src, q, up):
        return rdma(src, line.at[q], line_send.at[int(up), q], line_recv.at[q],
                    to(t, r + (1 if up else -1), c))

    def send_line(src, q, up):
        ok = (r < R - 1) if up else (r > 0)

        @pl.when(ok)
        def _():
            line_copy(src, q, up).start()

    def col_place(q):
        piece = q * C + c
        group = piece // n
        return lax.rem(group, T), group // T, lax.rem(piece, n)

    def col_copy(src, q):
        tt, cc, j = col_place(q)
        return rdma(src, col_ref.at[t, j], col_send.at[q], col_recv.at[t, j], to(tt, r, cc))

    def send_col(src, q):
        tt, cc, j = col_place(q)
        mine = jnp.logical_and(tt == t, cc == c)

        @pl.when(mine)
        def _():
            pltpu.make_async_copy(src, col_ref.at[t, j], col_recv.at[t, j]).start()

        @pl.when(jnp.logical_not(mine))
        def _():
            col_copy(src, q).start()

    own_out = pltpu.make_async_copy(x_ref, row_ref.at[t, c], local_sem)
    send_line(x_ref, r, True)
    send_line(x_ref, r, False)

    def row_copy(d):
        flat = lax.rem(t * chips + c // 2 + d, T * chips)
        return rdma(x_ref, row_ref.at[t, c], row_send.at[d], row_recv.at[d],
                    to(flat // chips, r, 2 * lax.rem(flat, chips) + core))

    for d in range(1, T * chips):
        row_copy(d).start()
    rdma(x_ref, row_ref.at[t, c], twin_send.at[0], twin_recv.at[0], to(t, r, twin)).start()
    own_out.start()
    send_col(x_ref, r)

    def row_arrived(d):
        flat = lax.rem(t * chips + c // 2 - d + T * chips, T * chips)
        slot = row_ref.at[flat // chips, 2 * lax.rem(flat, chips) + core]
        rdma(slot, slot, row_send.at[d], row_recv.at[d], to(t, r, twin)).wait_recv()
        rdma(slot, slot, twin_send.at[d], twin_recv.at[d], to(t, r, twin)).start()

    def line_arrived(dist):
        for up in (True, False):
            q = r - dist if up else r + dist
            ok = (q >= 0) if up else (q < R)

            @pl.when(ok)
            def _():
                line_copy(line.at[q], q, up).wait_recv()
                send_line(line.at[q], q, up)
                send_col(line.at[q], q)

    for dist in range(1, R):
        line_arrived(dist)
        if dist == 1:
            for d in range(1, T * chips):
                row_arrived(d)

    own_out.wait()
    for d in range(1, T * chips):
        row_copy(d).wait_send()
    for d in range(T * chips):
        flat = lax.rem(t * chips + c // 2 - d + T * chips, T * chips)
        mine = row_ref.at[flat // chips, 2 * lax.rem(flat, chips) + core]
        theirs = row_ref.at[flat // chips, 2 * lax.rem(flat, chips) + 1 - core]
        rdma(mine, mine, twin_send.at[d], twin_recv.at[d], to(t, r, twin)).wait_send()
        rdma(theirs, theirs, twin_send.at[d], twin_recv.at[d], to(t, r, twin)).wait_recv()
    for tt in range(T):
        for j in range(n):
            slot = col_ref.at[tt, j]
            pltpu.make_async_copy(slot, slot, col_recv.at[tt, j]).wait()
    for q in range(R):
        tt, cc, j = col_place(q)

        @pl.when(jnp.logical_not(jnp.logical_and(tt == t, cc == c)))
        def _():
            col_copy(x_ref, q).wait_send()

        @pl.when(jnp.logical_and(q <= r, r < R - 1))
        def _():
            line_copy(x_ref, q, True).wait_send()

        @pl.when(jnp.logical_and(q >= r, r > 0))
        def _():
            line_copy(x_ref, q, False).wait_send()


def gather(returns, T, R, C):
    days, width = returns.shape
    n = R // T
    dma = pltpu.SemaphoreType.DMA
    chips = T * C // 2
    return pl.pallas_call(
        functools.partial(gather_kernel, T, R, C),
        out_shape=(
            jax.ShapeDtypeStruct((T, C, days, width), returns.dtype),
            jax.ShapeDtypeStruct((T, n, days, width), returns.dtype),
        ),
        in_specs=[pl.BlockSpec(memory_space=pltpu.VMEM)],
        out_specs=(pl.BlockSpec(memory_space=pl.ANY), pl.BlockSpec(memory_space=pl.ANY)),
        scratch_shapes=[
            pltpu.VMEM((R, days, width), returns.dtype),
            dma((2, R)), dma((R,)),
            dma((chips,)), dma((chips,)),
            dma((chips,)), dma((chips,)),
            dma((R,)), dma((T, n)), dma,
        ],
        compiler_params=pltpu.CompilerParams(collective_id=0, has_side_effects=True),
    )(returns)


def corr_kernel(tile, depth, window_ref, out_ref_days, row_ref, col_ref, o_ref,
                rows_t, cols, col_a, col_m):
    i, k = pl.program_id(0), pl.program_id(1)
    K = out_ref_days.shape[0]
    T, n, half_days, width = col_ref.shape
    days = T * half_days
    extra = days - depth
    w = window_ref[0]
    wide = w.astype(jnp.float32)
    recip = 1.0 / wide

    def slot_mask(shape, dim, last):
        s = lax.broadcasted_iota(jnp.int32, shape, dim)
        day = jnp.where(s + depth <= last, s + depth, s)
        return (day <= last) & (day > last - w)

    def joined(ref, at):
        return jnp.concatenate([ref[tt, at] for tt in range(T)], axis=0)

    @pl.when((i == 0) & (k == 0))
    def _():
        for j in range(n):
            x = joined(col_ref, j)
            at = pl.ds(j * width, width)
            for kk in range(K):
                last = out_ref_days[kk]
                slot = lax.broadcasted_iota(jnp.int32, (extra, width), 0)
                head = jnp.where(slot + depth <= last, x[depth:].astype(jnp.float32),
                                 x[:extra].astype(jnp.float32)).astype(x.dtype)
                cols[kk, :extra, at] = head
                cols[kk, extra:, at] = x[extra:depth]
                f = jnp.where(slot_mask((depth, width), 0, last),
                              cols[kk, :, at].astype(jnp.float32), 0.0)
                first = jnp.sum(f, axis=0, keepdims=True)
                second = jnp.sum(f * f, axis=0, keepdims=True)
                scale = lax.rsqrt((second - first * first / wide) / wide + 1e-06)
                col_a[kk, :, at] = scale * recip
                col_m[kk, :, at] = first * recip * (scale * recip)

    per_piece = width // tile if width >= tile else 1

    @pl.when(k == 0)
    def _():
        piece = i // per_piece
        at = pl.ds(pl.multiple_of(lax.rem(i, per_piece) * tile, 128), tile)
        x = jnp.concatenate([row_ref[tt, piece, :, at] for tt in range(T)], axis=0)
        rows_t[:, :depth] = x[:depth].T
        tail = jnp.concatenate([x[depth:], jnp.zeros((128 - extra, tile), x.dtype)], axis=0)
        rows_t[:, depth:] = tail.T

    last = out_ref_days[k]
    lane = lax.broadcasted_iota(jnp.int32, (tile, 128), 1)
    use = (lane < extra) & (lane + depth <= last)
    head = jnp.where(use, rows_t[:, depth:].astype(jnp.float32), rows_t[:, :128].astype(jnp.float32))
    f = jnp.concatenate([head, rows_t[:, 128:depth].astype(jnp.float32)], axis=1)
    f = jnp.where(slot_mask((tile, depth), 1, last), f, 0.0)
    lhs = f.astype(jnp.bfloat16)
    first = jnp.sum(f, axis=1, keepdims=True)
    second = jnp.sum(f * f, axis=1, keepdims=True)
    scale = lax.rsqrt((second - first * first / wide) / wide + 1e-06)
    m = first * scale
    N = cols.shape[2]
    step = 256 if N % 256 == 0 else 128
    for b in range(0, N, step):
        g = jnp.dot(lhs, cols[k, :, b:b + step], preferred_element_type=jnp.float32)
        o = (g * scale) * col_a[k, :, b:b + step] - m * col_m[k, :, b:b + step]
        o_ref[0, :, b:b + step] = o.astype(o_ref.dtype)


def correlate(window, out_days, rows, cols):
    T, C, half_days, width = rows.shape
    n = cols.shape[1]
    K = out_days.shape[0]
    M, N = C * width, n * width
    depth = 256
    tile = min(512, width)
    grid_spec = pltpu.PrefetchScalarGridSpec(
        num_scalar_prefetch=2,
        grid=(M // tile, K),
        in_specs=[
            pl.BlockSpec(rows.shape, lambda i, k, *_: (0, 0, 0, 0)),
            pl.BlockSpec(cols.shape, lambda i, k, *_: (0, 0, 0, 0)),
        ],
        out_specs=pl.BlockSpec((1, tile, N), lambda i, k, *_: (k, i, 0)),
        scratch_shapes=[
            pltpu.VMEM((tile, depth + 128), jnp.bfloat16),
            pltpu.VMEM((K, depth, N), jnp.bfloat16),
            pltpu.VMEM((K, 1, N), jnp.float32),
            pltpu.VMEM((K, 1, N), jnp.float32),
        ],
    )
    return pl.pallas_call(
        functools.partial(corr_kernel, tile, depth),
        out_shape=jax.ShapeDtypeStruct((K, M, N), jnp.bfloat16),
        grid_spec=grid_spec,
        compiler_params=pltpu.CompilerParams(
            dimension_semantics=("arbitrary", "arbitrary"), vmem_limit_bytes=60 * 2**20),
    )(window, out_days, rows, cols)


def on_device(returns, window, out_days):
    T, R, C = lax.axis_size("tm"), lax.axis_size("row"), lax.axis_size("col")
    rows, cols = gather(returns, T, R, C)
    return correlate(window, out_days, rows, cols)


def solution(mesh):
    return jax.shard_map(
        on_device,
        mesh=mesh,
        in_specs=(P("tm", ("row", "col")), P(), P()),
        out_specs=P(None, "row", ("col", "tm")),
        check_vma=False,
    )
```

time: 273 us -> 80 us (0.29)
  waiting for transfers between devices: 174 us -> 0 us
  Pallas kernels: 0 us -> 79.1 us
  matrix products: 68.6 us -> 0 us
  between operations: 14.2 us -> 0.66 us
  blocking collectives: 12.4 us -> 0 us
    all_gather x2 -> x0, waiting for transfers between devices: 174 us -> none  [the longest x1 151 us: on_device(): everything = lax.all_gather(row_series, 'row', axis=1, tiled=True)]
    pallas_call x0 -> x2, Pallas kernels: none -> 79.1 us  [the longest x1 45.1 us: correlate(): pl.pallas_call(functools.partial(corr_kernel, tile, depth), out_shape=jax...]
    dot_general x5 -> x0, matrix products: 68.6 us -> none  [the longest x1 57.1 us: on_device(): jnp.einsum('kda,db->kab', weighted, col_series, preferred_element_type=jn...]
    all_gather x1 -> x0, blocking collectives: 12.4 us -> none  [on_device(): local = lax.all_gather(returns, 'tm', axis=0, tiled=True)]
  transfers between devices with their start and end apart: 2 -> 0, of which waited for: 2 -> 0; matrix products, arithmetic and copies ran while one was open for 3% -> 0% of each run, Pallas kernels for 0% -> 0%
where the time goes in v1:
time: 80 us; the launch traced here: 79.8 us
  Pallas kernels  79.1 us (99%)
    pallas_call x1, Pallas kernels, correlate(): pl.pallas_call(functools.partial(corr_kernel, tile, depth), out_shape=jax...  45.1 us
    pallas_call x1, Pallas kernels, gather(): pl.pallas_call(functools.partial(gather_kernel, T, R, C), out_shape=(jax....  34.1 us

profile of v1, /device:TPU:0, one launch (start us, length us, event | category | flops | bytes accessed | tf_op | source)
XLA Modules:
  0.0 79.8 jit_solution(9667385092392484808)
XLA Ops:
  0.7 34.1 %shard_map.37 = (bf16[2,4,136,1024]{3,2,1,0:T(8,128)(2,1)}, bf16[2,2,136,1024]{3,2,1,0:T(8,128)(2,1)}) custom-call(bf16[136,1024]{1,0:T(8,128)(2,1)} %x_ref.1), custom_call_target="tpu_custom_call" | custom-call | tf_op jit(solution)/shard_map/pallas_call | solution.py:148
  34.7 45.1 %shard_map.38 = bf16[4,4096,2048]{2,1,0:T(8,128)(2,1)} custom-call(s32[1]{0:T(128)S(6)} %copy.4.window_ref, s32[4]{0:T(128)} %out_ref_days.1, bf16[2,4,136,1024]{3,2,1,0:T(8,128)(2,1)} %get-tuple-element.7.row_ref, bf16[2,2,136,1024]{3,2,1,0:T(8,128)(2,1)} %get-tuple-element.8.col_ref), custom_call_target="tpu_custom_call" | custom-call | tf_op jit(solution)/shard_map/pallas_call | solution.py:258
